TPU v7x, 32 devices: a whole 2x2x4 slice. The times are simulated.
32 devices in a mesh: grp: 8 (over y, x, core), sub: 4 (over z).
Axes of the slice: x: 2, y: 2, z: 4, core: 2. Of those that a mesh axis runs over, the one named last changes fastest.
Arguments:
- master: float32 [4096, 3584], P(('grp', 'sub')), may hold values from -120 to 120
- moment_one: float32 [4096, 3584], P(('grp', 'sub')), may hold values from -6 to 6
- moment_two: float32 [4096, 3584], P(('grp', 'sub')), may hold values from 0.01 to 4
- gradient: float32 [4096, 3584], P(('grp', 'sub')), may hold values from -120 to 120
- partner: int32 [32], replicated, may hold values from 0 to 31, each once
- tensor_of_row: int32 [4096], replicated, may hold values from 0 to 7, never falling along the last dimension, each value on 1 to 1024 neighbouring positions
Outputs:
- new_master: float32 [4096, 3584], P(('grp', 'sub'))
- new_moment_one: float32 [4096, 3584], P(('grp', 'sub'))
- new_moment_two: float32 [4096, 3584], P(('grp', 'sub'))
Inputs may be any that keep to these rules, and one draw needn't show every extreme that they name: partner[n] is the device of new rank n; every device holds exactly one rank. `tensor_of_row`: tensor numbers never fall along the rows; each of the 8 tensors has one or more rows.
All inputs are finite; a program needn't handle non-finite values.
Results may differ from a plain program's by a relative error of at most 0.00007.
Values sent between devices are 32-bit elements; how exact they have to be, the bound alone decides.
A program may use at most 128 MiB of HBM per device.

v0:
```python
import jax
import jax.numpy as jnp
from jax import lax
from jax.sharding import PartitionSpec as P

LAYERS = 8
beta_one = 0.9
beta_two = 0.999
step_count = 10
adam_eps = 1e-06
trust_eps = 1e-06
learn_rate = 0.05
decay_rate = 0.01


def tensor_totals(values, onehot):
    return jnp.dot(values[None, :], onehot, precision=lax.Precision.HIGHEST)[0]


def local(master, moment_one, moment_two, gradient, partner, tensor_of_row):
    rows_dev, width = master.shape
    devices = lax.axis_size(("grp", "sub"))
    block = rows_dev // devices
    device_id = lax.axis_index(("grp", "sub"))
    numbers = jnp.arange(devices, dtype=jnp.int32)
    matches = partner[None, :] == numbers[:, None]
    inverse = jnp.sum(jnp.where(matches, numbers[None, :], 0), axis=1)
    my_rank = lax.dynamic_index_in_dim(inverse, device_id, 0, keepdims=False)
    layer_ids = jnp.arange(LAYERS, dtype=jnp.int32)
    id_grid = tensor_of_row.reshape(devices, devices, block)
    new_ids = lax.dynamic_index_in_dim(id_grid, my_rank, 1, keepdims=False).reshape(rows_dev)
    new_hot = (new_ids[:, None] == layer_ids[None, :]).astype(jnp.float32)
    old_ids = lax.dynamic_slice_in_dim(tensor_of_row, device_id * rows_dev, rows_dev)
    old_hot = (old_ids[:, None] == layer_ids[None, :]).astype(jnp.float32)
    weight_sq = lax.psum(tensor_totals(jnp.sum(master * master, axis=1), old_hot), ("grp", "sub"))

    def outbound(values):
        return jnp.take(values.reshape(devices, block, width), inverse, axis=0)

    sending = (outbound(master), outbound(moment_one), outbound(moment_two))
    arrived = (
        lax.all_to_all(sending[0], ("grp", "sub"), split_axis=0, concat_axis=0, tiled=True),
        lax.all_to_all(sending[1], ("grp", "sub"), split_axis=0, concat_axis=0, tiled=True),
        lax.all_to_all(sending[2], ("grp", "sub"), split_axis=0, concat_axis=0, tiled=True),
    )
    weights, moment_old, square_old = [piece.reshape(rows_dev, width) for piece in arrived]
    first = beta_one * moment_old + (1.0 - beta_one) * gradient
    second = beta_two * square_old + (1.0 - beta_two) * gradient * gradient
    correct_one = 1.0 - beta_one**step_count
    correct_two = 1.0 - beta_two**step_count
    update = (
        first / correct_one / (jnp.sqrt(second / correct_two) + adam_eps) + decay_rate * weights
    )
    update_local = tensor_totals(jnp.sum(update * update, axis=1), new_hot)
    update_sq = lax.psum(update_local, ("grp", "sub"))
    ratio = jnp.sqrt(weight_sq) / (jnp.sqrt(update_sq) + trust_eps)
    row_ratio = jnp.dot(new_hot, ratio[:, None], precision=lax.Precision.HIGHEST)
    fresh = weights - learn_rate * row_ratio * update
    return (fresh, first, second)


def solution(mesh):
    return jax.shard_map(
        local,
        mesh=mesh,
        in_specs=(
            P(("grp", "sub"), None),
            P(("grp", "sub"), None),
            P(("grp", "sub"), None),
            P(("grp", "sub"), None),
            P(),
            P(),
        ),
        out_specs=(P(("grp", "sub"), None), P(("grp", "sub"), None), P(("grp", "sub"), None)),
        check_vma=False,
    )
```

profile of v0, /device:TPU:0, one launch (start us, length us, event | category | flops | bytes accessed | tf_op | source)
XLA Modules:
  0.0 219.0 jit_solution(205470790843580463)
XLA Ops:
  0.6 0.8 select_reduce_fusion
  1.4 1.9 reshape.52
  3.3 2.8 %reshape.53 = f32[32,4,3584]{2,1,0:T(4,128)} reshape(f32[128,3584]{1,0:T(8,128)} %param.10) | data formatting | bytes 3670016 | tf_op jit(solution)/shard_map/reshape | solution.py:38
  6.2 2.8 %gather_fusion.1 = f32[32,4,3584]{2,1,0:T(4,128)} fusion(f32[32,4,3584]{2,1,0:T(4,128)S(1)} %reshape.52, s32[1024]{0:T(1024)S(1)} %pad_clamp_fusion), kind=kCustom, calls=%fused_computation.1.clone | custom fusion | bytes 3670144 | tf_op jit(solution)/shard_map/jit(_take)/gather | solution.py:38
  8.9 4.4 %gather_fusion.2 = f32[32,4,3584]{2,1,0:T(4,128)} fusion(f32[32,4,3584]{2,1,0:T(4,128)} %reshape.53, s32[1024]{0:T(1024)S(1)} %pad_clamp_fusion), kind=kCustom, calls=%fused_computation.2.clone | custom fusion | bytes 3670144 | tf_op jit(solution)/shard_map/jit(_take)/gather | solution.py:38
  13.3 0.0 copy-done.1
  13.3 1.8 reshape.49
  15.1 4.4 %gather_fusion = f32[32,4,3584]{2,1,0:T(4,128)} fusion(f32[32,4,3584]{2,1,0:T(4,128)} %reshape.49, s32[1024]{0:T(1024)S(1)} %pad_clamp_fusion), kind=kCustom, calls=%fused_computation.clone | custom fusion | bytes 3670144 | tf_op jit(solution)/shard_map/jit(_take)/gather | solution.py:38
  19.5 0.0 copy-done.2
  19.5 4.6 %broadcast_select_fusion = (f32[32,4,3584]{2,1,0:T(4,128)S(1)}, f32[32,4,3584]{2,1,0:T(4,128)S(1)}, f32[32,4,3584]{2,1,0:T(4,128)}) fusion(f32[32,4,3584]{2,1,0:T(4,128)} %gather_fusion.2, pred[32]{0:T(512)(128)(4,1)S(1)} %compare_and_fusion, f32[32,4,3584]{2,1,0:T(4,128)S(1)} %copy-done.2, f32[32,4,3584]{2,1,0:T(4,128)} %gather_fusion), kind=kLoop, calls=%fused_computation.14 | loop fusion | flops 1376256 | bytes 11010080 | tf_op jit(solution)/shard_map/jit(_take)/select_n | solution.py:38
  24.1 49.2 %all_to_all.15 = f32[32,4,3584]{2,1,0:T(4,128)} all-to-all(f32[32,4,3584]{2,1,0:T(4,128)S(1)} %get-tuple-element.9), channel_id=1, replica_groups=mesh['grp'=8,'sub'=4] {'grp','sub'}, dimensions={0} | all-to-all | bytes 3670016 | tf_op jit(solution)/shard_map/all_to_all | solution.py:44
  73.3 46.2 %all_to_all.16 = f32[32,4,3584]{2,1,0:T(4,128)S(1)} all-to-all(f32[32,4,3584]{2,1,0:T(4,128)S(1)} %get-tuple-element.10), channel_id=1, replica_groups=mesh['grp'=8,'sub'=4] {'grp','sub'}, dimensions={0} | all-to-all | bytes 3670016 | tf_op jit(solution)/shard_map/all_to_all | solution.py:43
  119.5 4.8 %all-to-all-start = ((f32[32,4,3584]{2,1,0:T(4,128)}), f32[32,4,3584]{2,1,0:T(4,128)}, u32[]{:S(2)}, u32[]{:S(2)}) async-start(f32[32,4,3584]{2,1,0:T(4,128)} %get-tuple-element.11), calls=%async_computation | async-start | bytes 3670016 | tf_op jit(solution)/shard_map/all_to_all | solution.py:42
  124.3 0.6 dynamic_slice.11
  126.2 0.5 reshape.51
  126.7 0.1 dynamic_slice.13
  127.5 0.1 dynamic-slice_reduce_fusion
  127.5 0.1 eq.44
  127.7 1.8 multiply_reduce_fusion.1
  129.5 0.2 convolution_bitcast_fusion.2
  129.7 0.0 copy-done
  129.7 1.7 broadcast_multiply_fusion
  131.4 2.9 %mul.76 = f32[128,3584]{1,0:T(8,128)} reshape(f32[32,4,3584]{2,1,0:T(4,128)} %broadcast_multiply_fusion) | data formatting | bytes 3670016 | tf_op jit(solution)/shard_map/mul | solution.py:48
  134.3 1.7 broadcast_multiply_fusion.1
  136.0 2.9 %mul.71 = f32[128,3584]{1,0:T(8,128)} reshape(f32[32,4,3584]{2,1,0:T(4,128)} %broadcast_multiply_fusion.1) | data formatting | bytes 3670016 | tf_op jit(solution)/shard_map/mul | solution.py:47
  138.9 26.5 %all-to-all-done = f32[32,4,3584]{2,1,0:T(4,128)} async-done(((f32[32,4,3584]{2,1,0:T(4,128)}), f32[32,4,3584]{2,1,0:T(4,128)}, u32[]{:S(2)}, u32[]{:S(2)}) %all-to-all-start) | async-done | bytes 1835040 | tf_op jit(solution)/shard_map/all_to_all | solution.py:42
  165.4 1.9 reshape.50
  167.3 5.7 %multiply_reduce_fusion = (f32[128]{0:T(128)S(1)}, f32[128,3584]{1,0:T(8,128)}, f32[128,3584]{1,0:T(8,128)}) fusion(f32[128,3584]{1,0:T(8,128)S(1)} %reshape.50, f32[128,3584]{1,0:T(8,128)} %mul.71, f32[128,3584]{1,0:T(8,128)} %param.11, f32[128,3584]{1,0:T(8,128)} %mul.76), kind=kLoop, calls=%fused_computation.6 | loop fusion | flops 5963648 | bytes 11010560 | tf_op jit(solution)/shard_map/reduce_sum | solution.py:54
  173.0 0.2 convolution_bitcast_fusion.1
  173.2 41.3 %all-reduce = (f32[8]{0:T(128)S(1)}, f32[8]{0:T(128)S(1)}) all-reduce(f32[8]{0:T(128)S(1)} %convolution_bitcast_fusion.1, f32[8]{0:T(128)S(1)} %convolution_bitcast_fusion.2), channel_id=1, replica_groups=mesh['grp'=8,'sub'=4] {'grp','sub'}, use_global_device_ids=true, to_apply=%region_4.6 | all-reduce | flops 16 | bytes 128 | tf_op jit(solution)/shard_map/psum | solution.py:55
  214.5 0.2 fusion.1
  214.7 4.3 %multiply_subtract_fusion = f32[128,3584]{1,0:T(8,128)} fusion(f32[128,3584]{1,0:T(8,128)S(1)} %reshape.50, f32[128]{0:T(128)S(1)} %fusion.1, f32[128,3584]{1,0:T(8,128)} %get-tuple-element.8, f32[128,3584]{1,0:T(8,128)} %get-tuple-element.7), kind=kLoop, calls=%fused_computation.5 | loop fusion | flops 3670016 | bytes 7340544 | tf_op jit(solution)/shard_map/sub | solution.py:58
  (8 shorter events, 0.0 us)
Async XLA Ops:
  8.9 4.4 %copy-start.1 = (f32[128,3584]{1,0:T(8,128)S(1)}, f32[128,3584]{1,0:T(8,128)}, u32[]{:S(2)}) copy-start(f32[128,3584]{1,0:T(8,128)} %param.8) | copy-start | bytes 5505028
  15.1 4.4 %copy-start.2 = (f32[32,4,3584]{2,1,0:T(4,128)S(1)}, f32[32,4,3584]{2,1,0:T(4,128)}, u32[]{:S(2)}) copy-start(f32[32,4,3584]{2,1,0:T(4,128)} %gather_fusion.1) | copy-start | bytes 5505028
  119.5 6.7 %copy-start.3 = (s32[4096]{0:T(1024)S(1)}, s32[4096]{0:T(1024)}, u32[]{:S(2)}) copy-start(s32[4096]{0:T(1024)} %param.13) | copy-start | bytes 49156
  119.5 45.8 %all-to-all-start = ((f32[32,4,3584]{2,1,0:T(4,128)}), f32[32,4,3584]{2,1,0:T(4,128)}, u32[]{:S(2)}, u32[]{:S(2)}) async-start(f32[32,4,3584]{2,1,0:T(4,128)} %get-tuple-element.11), calls=%async_computation | async-start | bytes 3670016 | tf_op jit(solution)/shard_map/all_to_all | solution.py:42
  127.6 2.1 copy-start
where the time goes:
time: 219 us
  blocking collectives  137 us (63%)
  local copies, waits for them, and re-layouts  27.1 us (12%)
  waiting for transfers between devices  26.5 us (12%)
  other arithmetic  20.7 us (9%)
  starting transfers between devices  4.76 us (2%)
  between operations  2.68 us (1%)
    all_to_all x1, blocking collectives, local(): lax.all_to_all(sending[2], ('grp', 'sub'), split_axis=0, concat_axis=0, t...  49.2 us
    all_to_all x1, blocking collectives, local(): lax.all_to_all(sending[1], ('grp', 'sub'), split_axis=0, concat_axis=0, t...  46.2 us
    psum x1, blocking collectives, local(): update_sq = lax.psum(update_local, ('grp', 'sub'))  41.3 us
    all_to_all x1, waiting for transfers between devices, local(): lax.all_to_all(sending[0], ('grp', 'sub'), split_axis=0, concat_axis=0, t...  26.5 us
    gather x3, local copies, waits for them, and re-layouts, outbound(): return jnp.take(values.reshape(devices, block, width), inverse, axis=0)  11.6 us
    reshape x3, local copies, waits for them, and re-layouts, outbound(): return jnp.take(values.reshape(devices, block, width), inverse, axis=0)  6.49 us
    reduce_sum x1, other arithmetic, local(): update_local = tensor_totals(jnp.sum(update * update, axis=1), new_hot)  5.68 us
    all_to_all x1, starting transfers between devices, local(): lax.all_to_all(sending[0], ('grp', 'sub'), split_axis=0, concat_axis=0, t...  4.76 us
  transfers between devices with their start and end apart: 1, of which 1 were waited for; matrix products, arithmetic and copies ran while one was open for 6% of the time, Pallas kernels for 0%

commit v1 on v0

--- a/solution.py
+++ b/solution.py
@@ -52,7 +52,7 @@
         first / correct_one / (jnp.sqrt(second / correct_two) + adam_eps) + decay_rate * weights
     )
     update_local = tensor_totals(jnp.sum(update * update, axis=1), new_hot)
-    update_sq = lax.psum(update_local, ("grp", "sub"))
+    update_sq = lax.psum(lax.psum(update_local, "sub"), "grp")
     ratio = jnp.sqrt(weight_sq) / (jnp.sqrt(update_sq) + trust_eps)
     row_ratio = jnp.dot(new_hot, ratio[:, None], precision=lax.Precision.HIGHEST)
     fresh = weights - learn_rate * row_ratio * update

time: 219 us -> 240 us (1.096)
  blocking collectives: 137 us -> 157 us
    psum x1 -> x3, blocking collectives: 41.3 us -> 61.7 us  [the longest x1 37 us: local(): lax.psum(tensor_totals(jnp.sum(master * master, axis=1), old_hot), ('grp'...]
  transfers between devices with their start and end apart: 1 -> 1, of which waited for: 1 -> 1; matrix products, arithmetic and copies ran while one was open for 6% -> 5% of each run, Pallas kernels for 0% -> 0%
where the time goes in v1:
time: 240 us
  blocking collectives  157 us (65%)
  local copies, waits for them, and re-layouts  27.3 us (11%)
  waiting for transfers between devices  26.5 us (11%)
  other arithmetic  20.7 us (9%)
  starting transfers between devices  4.76 us (2%)
  between operations  2.68 us (1%)
    all_to_all x1, blocking collectives, local(): lax.all_to_all(sending[2], ('grp', 'sub'), split_axis=0, concat_axis=0, t...  49.2 us
    all_to_all x1, blocking collectives, local(): lax.all_to_all(sending[1], ('grp', 'sub'), split_axis=0, concat_axis=0, t...  46.2 us
    psum x1, blocking collectives, local(): lax.psum(tensor_totals(jnp.sum(master * master, axis=1), old_hot), ('grp'...  37 us
    all_to_all x1, waiting for transfers between devices, local(): lax.all_to_all(sending[0], ('grp', 'sub'), split_axis=0, concat_axis=0, t...  26.5 us
    psum x2, blocking collectives, local(): update_sq = lax.psum(lax.psum(update_local, 'sub'), 'grp')  24.7 us
    gather x3, local copies, waits for them, and re-layouts, outbound(): return jnp.take(values.reshape(devices, block, width), inverse, axis=0)  11.6 us
    reshape x3, local copies, waits for them, and re-layouts, outbound(): return jnp.take(values.reshape(devices, block, width), inverse, axis=0)  6.49 us
    reduce_sum x1, other arithmetic, local(): update_local = tensor_totals(jnp.sum(update * update, axis=1), new_hot)  5.68 us
  transfers between devices with their start and end apart: 1, of which 1 were waited for; matrix products, arithmetic and copies ran while one was open for 5% of the time, Pallas kernels for 0%

profile of v1, /device:TPU:0, one launch (start us, length us, event | category | flops | bytes accessed | tf_op | source)
XLA Modules:
  0.0 239.6 jit_solution(2474067026728267458)
XLA Ops:
  0.6 0.8 select_reduce_fusion
  1.4 1.9 reshape.52
  3.3 2.8 %reshape.53 = f32[32,4,3584]{2,1,0:T(4,128)} reshape(f32[128,3584]{1,0:T(8,128)} %param.10) | data formatting | bytes 3670016 | tf_op jit(solution)/shard_map/reshape | solution.py:38
  6.2 2.8 %gather_fusion.1 = f32[32,4,3584]{2,1,0:T(4,128)} fusion(f32[32,4,3584]{2,1,0:T(4,128)S(1)} %reshape.52, s32[1024]{0:T(1024)S(1)} %pad_clamp_fusion), kind=kCustom, calls=%fused_computation.1.clone | custom fusion | bytes 3670144 | tf_op jit(solution)/shard_map/jit(_take)/gather | solution.py:38
  8.9 4.4 %gather_fusion.2 = f32[32,4,3584]{2,1,0:T(4,128)} fusion(f32[32,4,3584]{2,1,0:T(4,128)} %reshape.53, s32[1024]{0:T(1024)S(1)} %pad_clamp_fusion), kind=kCustom, calls=%fused_computation.2.clone | custom fusion | bytes 3670144 | tf_op jit(solution)/shard_map/jit(_take)/gather | solution.py:38
  13.3 1.8 reshape.49
  15.1 4.4 %gather_fusion = f32[32,4,3584]{2,1,0:T(4,128)} fusion(f32[32,4,3584]{2,1,0:T(4,128)} %reshape.49, s32[1024]{0:T(1024)S(1)} %pad_clamp_fusion), kind=kCustom, calls=%fused_computation.clone | custom fusion | bytes 3670144 | tf_op jit(solution)/shard_map/jit(_take)/gather | solution.py:38
  19.5 4.6 %broadcast_select_fusion = (f32[32,4,3584]{2,1,0:T(4,128)S(1)}, f32[32,4,3584]{2,1,0:T(4,128)S(1)}, f32[32,4,3584]{2,1,0:T(4,128)}) fusion(f32[32,4,3584]{2,1,0:T(4,128)} %gather_fusion.2, pred[32]{0:T(512)(128)(4,1)S(1)} %compare_and_fusion, f32[32,4,3584]{2,1,0:T(4,128)S(1)} %copy-done.2, f32[32,4,3584]{2,1,0:T(4,128)} %gather_fusion), kind=kLoop, calls=%fused_computation.14 | loop fusion | flops 1376256 | bytes 11010080 | tf_op jit(solution)/shard_map/jit(_take)/select_n | solution.py:38
  24.1 49.2 %all_to_all.15 = f32[32,4,3584]{2,1,0:T(4,128)} all-to-all(f32[32,4,3584]{2,1,0:T(4,128)S(1)} %get-tuple-element.7), channel_id=1, replica_groups=mesh['grp'=8,'sub'=4] {'grp','sub'}, dimensions={0} | all-to-all | bytes 3670016 | tf_op jit(solution)/shard_map/all_to_all | solution.py:44
  73.3 46.2 %all_to_all.16 = f32[32,4,3584]{2,1,0:T(4,128)S(1)} all-to-all(f32[32,4,3584]{2,1,0:T(4,128)S(1)} %get-tuple-element.8), channel_id=1, replica_groups=mesh['grp'=8,'sub'=4] {'grp','sub'}, dimensions={0} | all-to-all | bytes 3670016 | tf_op jit(solution)/shard_map/all_to_all | solution.py:43
  119.5 4.8 %all-to-all-start = ((f32[32,4,3584]{2,1,0:T(4,128)}), f32[32,4,3584]{2,1,0:T(4,128)}, u32[]{:S(2)}, u32[]{:S(2)}) async-start(f32[32,4,3584]{2,1,0:T(4,128)} %get-tuple-element.9), calls=%async_computation | async-start | bytes 3670016 | tf_op jit(solution)/shard_map/all_to_all | solution.py:42
  124.3 0.6 dynamic_slice.11
  126.2 0.5 reshape.51
  126.7 0.1 dynamic_slice.13
  127.5 0.1 dynamic-slice_reduce_fusion
  127.5 0.1 eq.44
  127.7 1.8 multiply_reduce_fusion.1
  129.5 0.2 copy-done
  129.7 1.7 broadcast_multiply_fusion
  131.4 2.9 %mul.76 = f32[128,3584]{1,0:T(8,128)} reshape(f32[32,4,3584]{2,1,0:T(4,128)} %broadcast_multiply_fusion) | data formatting | bytes 3670016 | tf_op jit(solution)/shard_map/mul | solution.py:48
  134.3 1.7 broadcast_multiply_fusion.1
  136.0 2.9 %mul.71 = f32[128,3584]{1,0:T(8,128)} reshape(f32[32,4,3584]{2,1,0:T(4,128)} %broadcast_multiply_fusion.1) | data formatting | bytes 3670016 | tf_op jit(solution)/shard_map/mul | solution.py:47
  138.9 26.5 %all-to-all-done = f32[32,4,3584]{2,1,0:T(4,128)} async-done(((f32[32,4,3584]{2,1,0:T(4,128)}), f32[32,4,3584]{2,1,0:T(4,128)}, u32[]{:S(2)}, u32[]{:S(2)}) %all-to-all-start) | async-done | bytes 1835040 | tf_op jit(solution)/shard_map/all_to_all | solution.py:42
  165.4 1.9 reshape.50
  167.3 5.7 %multiply_reduce_fusion = (f32[128]{0:T(128)S(1)}, f32[128,3584]{1,0:T(8,128)}, f32[128,3584]{1,0:T(8,128)}) fusion(f32[128,3584]{1,0:T(8,128)S(1)} %reshape.50, f32[128,3584]{1,0:T(8,128)} %mul.71, f32[128,3584]{1,0:T(8,128)} %param.11, f32[128,3584]{1,0:T(8,128)} %mul.76), kind=kLoop, calls=%fused_computation.6 | loop fusion | flops 5963648 | bytes 11010560 | tf_op jit(solution)/shard_map/reduce_sum | solution.py:54
  173.0 0.2 convolution_bitcast_fusion.1
  173.2 0.2 convolution_bitcast_fusion.2
  173.4 12.0 %psum.22 = f32[8]{0:T(128)S(1)} all-reduce(f32[8]{0:T(128)S(1)} %convolution_bitcast_fusion.1), channel_id=1, replica_groups=mesh['grp'=8,'sub'=4] {'sub'}, use_global_device_ids=true, to_apply=%region_4.6 | all-reduce | flops 8 | bytes 64 | tf_op jit(solution)/shard_map/psum | solution.py:55
  185.4 37.0 %psum.21 = f32[8]{0:T(128)S(1)} all-reduce(f32[8]{0:T(128)S(1)} %convolution_bitcast_fusion.2), channel_id=1, replica_groups=mesh['grp'=8,'sub'=4] {'grp','sub'}, use_global_device_ids=true, to_apply=%region_2.4 | all-reduce | flops 8 | bytes 64 | tf_op jit(solution)/shard_map/psum | solution.py:35
  222.4 12.7 %psum.23 = f32[8]{0:T(128)S(1)} all-reduce(f32[8]{0:T(128)S(1)} %psum.22), channel_id=1, replica_groups=mesh['grp'=8,'sub'=4] {'grp'}, use_global_device_ids=true, to_apply=%region_5.7 | all-reduce | flops 8 | bytes 64 | tf_op jit(solution)/shard_map/psum | solution.py:55
  235.1 0.2 fusion.1
  235.3 4.3 %multiply_subtract_fusion = f32[128,3584]{1,0:T(8,128)} fusion(f32[128,3584]{1,0:T(8,128)S(1)} %reshape.50, f32[128]{0:T(128)S(1)} %fusion.1, f32[128,3584]{1,0:T(8,128)} %get-tuple-element.6, f32[128,3584]{1,0:T(8,128)} %get-tuple-element.5), kind=kLoop, calls=%fused_computation.5 | loop fusion | flops 3670016 | bytes 7340544 | tf_op jit(solution)/shard_map/sub | solution.py:58
  (10 shorter events, 0.0 us)
Async XLA Ops:
  8.9 4.4 %copy-start.1 = (f32[128,3584]{1,0:T(8,128)S(1)}, f32[128,3584]{1,0:T(8,128)}, u32[]{:S(2)}) copy-start(f32[128,3584]{1,0:T(8,128)} %param.8) | copy-start | bytes 5505028
  15.1 4.4 %copy-start.2 = (f32[32,4,3584]{2,1,0:T(4,128)S(1)}, f32[32,4,3584]{2,1,0:T(4,128)}, u32[]{:S(2)}) copy-start(f32[32,4,3584]{2,1,0:T(4,128)} %gather_fusion.1) | copy-start | bytes 5505028
  119.5 6.7 %copy-start.3 = (s32[4096]{0:T(1024)S(1)}, s32[4096]{0:T(1024)}, u32[]{:S(2)}) copy-start(s32[4096]{0:T(1024)} %param.13) | copy-start | bytes 49156
  119.5 45.8 %all-to-all-start = ((f32[32,4,3584]{2,1,0:T(4,128)}), f32[32,4,3584]{2,1,0:T(4,128)}, u32[]{:S(2)}, u32[]{:S(2)}) async-start(f32[32,4,3584]{2,1,0:T(4,128)} %get-tuple-element.9), calls=%async_computation | async-start | bytes 3670016 | tf_op jit(solution)/shard_map/all_to_all | solution.py:42
  127.6 2.1 copy-start
